TPU v7x, 128 devices: a whole 4x4x4 slice. The times are simulated.
128 devices in a mesh: ta: 2 (over core), ha: 2 (over z_hi), wa: 32 (over z_lo, x, y).
Axes of the slice: x: 4, y: 4, z: 4 (z_hi: 2, z_lo: 2; z = z_hi * 2 + z_lo), core: 2. Of those that a mesh axis runs over, the one named last changes fastest.
Arguments:
- features: bfloat16 [2, 16, 28, 448, 1024], P(None, 'ta', 'ha', 'wa'), may hold values from -6 to 6
- teacher: bfloat16 [2, 16, 28, 448, 1000], P(None, 'ta', 'ha', 'wa'), may hold values from -30 to 750
- head_weight: float32 [1024, 1000], replicated, may hold values from -0.1875 to 0.1875
Outputs:
- feature_grad: bfloat16 [2, 16, 28, 448, 1024], P(None, 'ta', 'ha', 'wa')
- loss: float32 [], replicated
- new_weight: float32 [1024, 1000], P(('ta', 'ha', 'wa'))
All inputs are finite; a program needn't handle non-finite values.
Results may differ from a plain program's by a relative error of at most 0.0056.
Values may be sent and summed in bfloat16 or wider, within the bound.
No kernel may reach another device: no remote copies, remote signals or barrier semaphores. Data moves between devices by JAX's collectives and lax.ppermute only.
A program may use at most 192 MiB of HBM per device.

v0:
```python
import jax
import jax.numpy as jnp
from jax import lax
from jax.sharding import PartitionSpec as P

WW = 14
WV = 28


sharpness_divisor = 2.0
learn_rate = 0.1
clip_norm = 1000.0


def with_halo(block, sides, width):
    for axis, dim in sides:
        count = lax.axis_size(axis)
        forward = [(i, i + 1) for i in range(count - 1)]
        backward = [(target, source) for source, target in forward]
        low = lax.ppermute(
            lax.slice_in_dim(block, block.shape[dim] - width, None, axis=dim), axis, forward
        )
        high = lax.ppermute(lax.slice_in_dim(block, 0, width, axis=dim), axis, backward)
        block = jnp.concatenate([low, block, high], axis=dim)
    return block


def three_sum(padded, reduce_dimension, length):
    first = lax.slice_in_dim(padded, 0, length, axis=reduce_dimension)
    middle = lax.slice_in_dim(padded, 1, length + 1, axis=reduce_dimension)
    last = lax.slice_in_dim(padded, 2, length + 2, axis=reduce_dimension)
    return first + middle + last


def edge_count(position, length):
    return 3.0 - (position == 0).astype(jnp.float32) - (position == length - 1).astype(jnp.float32)


def clip_of(columns):
    return (columns + WV - WW // 2) // WV


def local(features, teacher, head_weight):
    batch, frames, rows, columns, width = features.shape
    classes = teacher.shape[-1]
    grid_wide = columns * lax.axis_size("wa")
    time_index = lax.axis_index("ta")
    height_index = lax.axis_index("ha")
    width_index = lax.axis_index("wa")
    frame_pos = time_index * frames + jnp.arange(frames, dtype=jnp.int32)
    row_pos = height_index * rows + jnp.arange(rows, dtype=jnp.int32)
    column_pos = width_index * columns + jnp.arange(columns, dtype=jnp.int32)
    own_clip = clip_of(column_pos)
    left_ok = (
        ((column_pos > 0) & (clip_of(column_pos - 1) == own_clip))
        .astype(jnp.float32)
        .reshape(1, 1, 1, columns, 1)
    )
    right_ok = (
        ((column_pos < grid_wide - 1) & (clip_of(column_pos + 1) == own_clip))
        .astype(jnp.float32)
        .reshape(1, 1, 1, columns, 1)
    )
    counts = (
        edge_count(frame_pos, frames * lax.axis_size("ta")).reshape(1, frames, 1, 1, 1)
        * edge_count(row_pos, rows * lax.axis_size("ha")).reshape(1, 1, rows, 1, 1)
        * (1.0 + left_ok + right_ok)
    )
    padded = with_halo(teacher, (("ta", 1), ("ha", 2), ("wa", 3)), 1)
    summed = three_sum(padded.astype(jnp.float32), 1, frames)
    summed = three_sum(summed, 2, rows)
    summed = (
        summed[:, :, :, 0:columns] * left_ok
        + summed[:, :, :, 1 : columns + 1]
        + summed[:, :, :, 2 : columns + 2] * right_ok
    )
    averaged_scores = (summed / counts).reshape(-1, classes)
    head_bf = head_weight.astype(jnp.bfloat16)
    feat_rows = features.reshape(-1, width)
    pupil_scores = jnp.dot(feat_rows, head_bf, preferred_element_type=jnp.float32)
    pupil_entropy_terms = jax.nn.log_softmax(pupil_scores / sharpness_divisor, axis=-1)
    mentor_entropy_terms = jax.nn.log_softmax(averaged_scores / sharpness_divisor, axis=-1)
    mentor_likelihoods = jnp.exp(mentor_entropy_terms)
    pupil_likelihoods = jnp.exp(pupil_entropy_terms)
    patch_kullback_leibler = jnp.sum(
        mentor_likelihoods * (mentor_entropy_terms - pupil_entropy_terms), axis=-1
    )
    piece_objective = sharpness_divisor * sharpness_divisor * jnp.sum(patch_kullback_leibler)
    score_slope = (sharpness_divisor * (pupil_likelihoods - mentor_likelihoods)).astype(
        jnp.bfloat16
    )
    feat_grad = lax.dot_general(
        score_slope, head_bf, (((1,), (1,)), ((), ())), preferred_element_type=jnp.float32
    )
    feature_grad = feat_grad.astype(jnp.bfloat16).reshape(features.shape)
    owned = width // lax.axis_size(("ta", "ha", "wa"))
    first_row = lax.axis_index(("ta", "ha", "wa")) * owned
    local_grad = lax.dot_general(
        feat_rows, score_slope, (((0,), (0,)), ((), ())), preferred_element_type=jnp.float32
    )
    head_grad, loss = lax.psum((local_grad, piece_objective), ("ta", "ha", "wa"))
    squares = jnp.sum(head_grad * head_grad)
    mine = lax.dynamic_slice_in_dim(head_grad, first_row, owned, 0)
    grad_norm = jnp.sqrt(squares)
    clip = jnp.minimum(1.0, clip_norm / (grad_norm + 1e-06))
    weight_rows = lax.dynamic_slice_in_dim(head_weight, first_row, owned, 0)
    new_weight = weight_rows - learn_rate * clip * mine
    return (feature_grad, loss, new_weight)


def solution(mesh):
    placed = (P(None, "ta", "ha", "wa", None), P(None, "ta", "ha", "wa", None), P())
    return jax.shard_map(
        local,
        mesh=mesh,
        in_specs=placed,
        out_specs=(P(None, "ta", "ha", "wa", None), P(), P(("ta", "ha", "wa"), None)),
        check_vma=False,
    )
```

profile of v0, /device:TPU:1, one launch (start us, length us, event | category | flops | bytes accessed | tf_op | source)
XLA Modules:
  0.0 399.8 jit_solution(7508793747591281292)
XLA Ops:
  7.2 8.3 %fusion.11 = (bf16[2,1,14,14,1000]{4,1,3,2,0:T(2,128)(2,1)S(1)}, bf16[2,1,14,14,1000]{4,1,3,2,0:T(2,128)(2,1)S(1)}) fusion(bf16[2,8,14,14,1000]{4,1,3,2,0:T(8,128)(2,1)} %param.5), kind=kLoop, calls=%fused_computation.51 | loop fusion | bytes 3136000 | tf_op jit(solution)/shard_map/slice | solution.py:23
  15.5 1.3 copy.26
  16.8 1.3 collective-permute-start
  18.0 1.2 copy.27
  19.3 3.4 collective-permute-start.1
  22.7 6.7 %copy.14 = bf16[2,8,14,14,1024]{4,3,2,1,0:T(8,128)(2,1)} copy(bf16[2,8,14,14,1024]{4,1,3,2,0:T(8,128)(2,1)S(1)} %copy-done.2) | data formatting | bytes 12845056 | tf_op args[0]
  29.4 10.1 %reshape.134 = bf16[3136,1024]{1,0:T(8,128)(2,1)} reshape(bf16[2,8,14,14,1024]{4,3,2,1,0:T(8,128)(2,1)} %copy.14) | data formatting | bytes 12845056 | tf_op jit(solution)/shard_map/reshape | solution.py:79
  39.5 11.1 %multiply_reduce_fusion.1 = (f32[3136]{0:T(1024)S(1)}, f32[3136,1000]{0,1:T(8,128)S(1)}) fusion(bf16[3136,1024]{1,0:T(8,128)(2,1)} %reshape.134, f32[1024,1000]{0,1:T(8,128)} %param.6), kind=kOutput, calls=%fused_computation.15 | convolution fusion | flops 6429820928 | bytes 23075072 | tf_op jit(solution)/shard_map/dot_general | solution.py:80
  50.6 1.1 constant_dynamic-update-slice_fusion.2
  51.7 13.1 %constant_dynamic-update-slice_fusion.1 = bf16[2,10,14,14,1000]{4,3,2,1,0:T(8,128)(2,1)} fusion(bf16[2,10,14,14,1000]{4,3,2,1,0:T(8,128)(2,1)} %constant_dynamic-update-slice_fusion.2, bf16[2,8,14,14,1000]{4,1,3,2,0:T(8,128)(2,1)} %param.5), kind=kLoop, calls=%fused_computation.30 | loop fusion | bytes 13762560
  64.9 1.1 constant_dynamic-update-slice_fusion
  65.9 2.5 fusion.10
  68.4 6.1 %collective-permute-start.2 = (bf16[2,10,1,14,1000]{4,3,2,1,0:T(8,128)(2,1)}, bf16[2,10,1,14,1000]{4,3,2,1,0:T(8,128)(2,1)S(1)}, u32[]{:S(2)}, u32[]{:S(2)}) collective-permute-start(bf16[2,10,1,14,1000]{4,3,2,1,0:T(8,128)(2,1)} %get-tuple-element.17), channel_id=1, source_target_pairs={{0,32},{1,33},{2,34},{3,35},{4,36},{5,37},{6,38},{7,39},{8,40},{9,... | collective-permute-start | bytes 1680008 | tf_op jit(solution)/shard_map/ppermute | solution.py:20
  74.5 1.3 collective-permute-start.3
  75.8 2.1 exponential_reduce_fusion.1
  78.0 11.1 %collective-permute-done.2 = bf16[2,10,1,14,1000]{4,3,2,1,0:T(8,128)(2,1)S(1)} collective-permute-done((bf16[2,10,1,14,1000]{4,3,2,1,0:T(8,128)(2,1)}, bf16[2,10,1,14,1000]{4,3,2,1,0:T(8,128)(2,1)S(1)}, u32[]{:S(2)}, u32[]{:S(2)}) %collective-permute-start.2) | collective-permute-done | bytes 560032 | tf_op jit(solution)/shard_map/ppermute | solution.py:20
  89.1 5.7 %collective-permute-done.3 = bf16[2,10,1,14,1000]{4,3,2,1,0:T(8,128)(2,1)S(1)} collective-permute-done((bf16[2,10,1,14,1000]{4,3,2,1,0:T(8,128)(2,1)}, bf16[2,10,1,14,1000]{4,3,2,1,0:T(8,128)(2,1)S(1)}, u32[]{:S(2)}, u32[]{:S(2)}) %collective-permute-start.3) | collective-permute-done | bytes 560032 | tf_op jit(solution)/shard_map/ppermute | solution.py:23
  94.8 6.0 %pad_maximum_fusion.2 = (bf16[2,10,16,1,1000]{4,3,2,1,0:T(2,128)(2,1)S(1)}, bf16[2,10,16,1,1000]{4,3,2,1,0:T(2,128)(2,1)S(1)}) fusion(bf16[2,10,1,14,1000]{4,3,2,1,0:T(8,128)(2,1)S(1)} %collective-permute-done.3, bf16[2,10,14,14,1000]{4,3,2,1,0:T(8,128)(2,1)} %constant_dynamic-update-slice_fusion, bf16[2,10,1,14,1000]{4,3,2,1,0:T(8,128)(2,1)S(1)} %collective-permute-done.2), kind=kLoop, calls=%fused_computation.23 | loop fusion | flops 3840000 | bytes 10240000 | tf_op jit(solution)/shard_map/slice | solution.py:21
  100.8 0.2 copy.18
  101.0 3.2 collective-permute-start.4
  104.3 0.2 copy.19
  104.5 1.3 collective-permute-start.5
  105.9 0.1 broadcast_multiply_fusion.1
  105.9 0.1 broadcast_multiply_fusion
  106.0 11.8 %collective-permute-done.4 = bf16[2,10,16,1,1000]{4,2,3,1,0:T(8,128)(2,1)S(1)} collective-permute-done((bf16[2,10,16,1,1000]{4,2,3,1,0:T(8,128)(2,1)S(1)}, bf16[2,10,16,1,1000]{4,2,3,1,0:T(8,128)(2,1)S(1)}, u32[]{:S(2)}, u32[]{:S(2)}) %collective-permute-start.4) | collective-permute-done | bytes 640032 | tf_op jit(solution)/shard_map/ppermute | solution.py:20
  117.8 1.2 copy.20
  119.0 2.9 collective-permute-done.5
  121.9 1.2 copy.21
  123.2 7.9 %maximum_convert_fusion = f32[2,10,16,16,1000]{4,3,2,1,0:T(8,128)S(1)} fusion(bf16[2,10,16,1,1000]{4,3,2,1,0:T(2,128)(2,1)S(1)} %copy.21, bf16[2,10,1,14,1000]{4,3,2,1,0:T(8,128)(2,1)S(1)} %collective-permute-done.3, bf16[2,10,14,14,1000]{4,3,2,1,0:T(8,128)(2,1)S(1)} %bitcast.7, bf16[2,10,1,14,1000]{4,3,2,1,0:T(8,128)(2,1)S(1)} %collective-permute-done.2, ...), kind=kLoop, calls=%fused_computation.17 | loop fusion | flops 51200000 | bytes 30720000 | tf_op jit(solution)/shard_map/convert_element_type | solution.py:70
  131.1 9.0 %slice_add_fusion = f32[2,8,16,16,1000]{4,3,2,1,0:T(8,128)} fusion(f32[2,10,16,16,1000]{4,3,2,1,0:T(8,128)S(1)} %maximum_convert_fusion), kind=kLoop, calls=%fused_computation | loop fusion | flops 8192000 | bytes 65536000 | tf_op jit(solution)/shard_map/add | solution.py:32
  140.1 15.5 %slice_add_fusion.3 = f32[2,8,14,16,1000]{4,3,2,1,0:T(8,128)S(1)} fusion(f32[2,8,16,16,1000]{4,3,2,1,0:T(8,128)} %slice_add_fusion), kind=kLoop, calls=%fused_computation.8 | loop fusion | flops 7168000 | bytes 57344000 | tf_op jit(solution)/shard_map/add | solution.py:32
  155.6 9.3 %fusion.2 = f32[2,8,14,14,1000]{4,3,2,1,0:T(8,128)} fusion(f32[2,8,14,16,1000]{4,3,2,1,0:T(8,128)S(1)} %slice_add_fusion.3, f32[8,14,14]{2,1,0:T(8,128)S(1)} %broadcast_multiply_fusion, f32[14]{0:T(128)S(1)} %get-tuple-element.23, f32[14]{0:T(128)S(1)} %get-tuple-element.24), kind=kLoop, calls=%fused_computation.5 | loop fusion | flops 18816000 | bytes 50182384 | tf_op jit(solution)/shard_map/div | solution.py:82
  164.9 14.4 %div.64 = f32[3136,1000]{1,0:T(8,128)} reshape(f32[2,8,14,14,1000]{4,3,2,1,0:T(8,128)} %fusion.2) | data formatting | bytes 25088000 | tf_op jit(solution)/shard_map/div | solution.py:82
  179.3 13.3 %copy.22 = f32[3136,1000]{0,1:T(8,128)} copy(f32[3136,1000]{1,0:T(8,128)} %div.64) | data formatting | bytes 25088000 | tf_op jit(solution)/shard_map/div | solution.py:82
  192.6 5.3 %reduce_max.14 = f32[3136]{0:T(1024)S(1)} reduce(f32[3136,1000]{1,0:T(8,128)} %div.64, f32[]{:T(128)} %constant.26.clone.2), dimensions={1}, to_apply=%region_0.1.clone | reduce | flops 3132864 | bytes 12556548 | tf_op jit(solution)/shard_map/jit(log_softmax)/reduce_max | solution.py:82
  197.9 6.5 %exponential_reduce_fusion = f32[3136]{0:T(1024)S(1)} fusion(f32[3136,1000]{0,1:T(8,128)} %copy.22, f32[3136]{0:T(1024)S(1)} %reduce_max.14), kind=kLoop, calls=%fused_computation.10 | loop fusion | flops 6268864 | bytes 12569088 | tf_op jit(solution)/shard_map/jit(log_softmax)/reduce_sum | solution.py:82
  204.5 1.7 copy-done
  206.2 9.3 %multiply_reduce_fusion = (f32[]{:T(128)}, bf16[3136,1000]{0,1:T(8,128)(2,1)S(1)}) fusion(f32[3136,1000]{0,1:T(8,128)S(1)} %copy-done, f32[3136,1000]{0,1:T(8,128)} %copy-done.1, f32[3136]{0:T(1024)S(1)} %log.10, f32[3136]{0:T(1024)S(1)} %reduce_max.14, f32[3136]{0:T(1024)S(1)} %log.9, f32[3136]{0:T(1024)S(1)} %get-tuple-element.21), kind=kLoop, calls=%fused_computation.12 | loop fusion | flops 34496000 | bytes 31410180 | tf_op jit(solution)/shard_map/reduce_sum | solution.py:88
  215.5 2.7 copy-done.3
  218.2 10.7 %convolution_bitcast_fusion = f32[1024,1000]{0,1:T(8,128)} fusion(bf16[3136,1000]{0,1:T(8,128)(2,1)S(1)} %get-tuple-element.14, bf16[3136,1024]{1,0:T(8,128)(2,1)} %reshape.134), kind=kOutput, calls=%fused_computation.20 | convolution fusion | flops 6422528000 | bytes 16790528 | tf_op jit(solution)/shard_map/dot_general | solution.py:98
  229.6 68.8 %psum.14 = f32[]{:T(128)} all-reduce(f32[]{:T(128)S(6)} %mul_shard_map.6), channel_id=1, replica_groups=mesh['ta'=2,'ha'=2,'wa'=32] {'ta','ha','wa'}, use_global_device_ids=true, to_apply=%region_3.5 | all-reduce | flops 1 | bytes 8 | tf_op jit(solution)/shard_map/psum | solution.py:101
  298.4 12.3 %convolution_convert_fusion = bf16[3136,1024]{1,0:T(8,128)(2,1)} fusion(bf16[3136,1000]{0,1:T(8,128)(2,1)} %copy-done.3, f32[1024,1000]{0,1:T(8,128)} %param.6), kind=kOutput, calls=%fused_computation.18 | convolution fusion | flops 6426763264 | bytes 16790528 | tf_op jit(solution)/shard_map/dot_general | solution.py:92
  310.7 10.0 %reshape.135 = bf16[2,8,14,14,1024]{4,3,2,1,0:T(8,128)(2,1)} reshape(bf16[3136,1024]{1,0:T(8,128)(2,1)} %convolution_convert_fusion) | data formatting | bytes 12845056 | tf_op jit(solution)/shard_map/reshape | solution.py:95
  320.7 10.7 %copy.23 = bf16[2,8,14,14,1024]{4,1,3,2,0:T(8,128)(2,1)} copy(bf16[2,8,14,14,1024]{4,3,2,1,0:T(8,128)(2,1)} %reshape.135) | data formatting | bytes 12845056
  331.4 54.5 %all-reduce.2.cloned.1.call-done = f32[1024,1000]{0,1:T(8,128)} async-done(((f32[1024,1000]{0,1:T(8,128)}), f32[1024,1000]{0,1:T(8,128)}) %all-reduce.2.cloned.1.call-update) | async-done | bytes 4096016 | tf_op jit(solution)/shard_map/psum | solution.py:101
  385.8 3.8 multiply_reduce_fusion.2
  390.4 1.5 multiply_subtract_fusion.1
  391.9 0.8 copy.24
  (23 shorter events, 0.2 us)
Async XLA Ops:
  7.2 378.7 %all-reduce.2.cloned.1.call-start = ((), (), s32[]{:S(2)}) async-start(), calls=%async_computation | async-start | bytes 8192000 | tf_op jit(solution)/shard_map/psum | solution.py:101
  7.2 15.5 %copy-start.2 = (bf16[2,8,14,14,1024]{4,1,3,2,0:T(8,128)(2,1)S(1)}, bf16[2,8,14,14,1024]{4,1,3,2,0:T(8,128)(2,1)}, u32[]{:S(2)}) copy-start(bf16[2,8,14,14,1024]{4,1,3,2,0:T(8,128)(2,1)} %param.4) | copy-start | bytes 19267588
  16.8 33.9 %collective-permute-start = (bf16[2,1,14,14,1000]{4,3,2,1,0:T(8,128)(2,1)}, bf16[2,1,14,14,1000]{4,3,2,1,0:T(8,128)(2,1)S(1)}, u32[]{:S(2)}, u32[]{:S(2)}) collective-permute-start(bf16[2,1,14,14,1000]{4,3,2,1,0:T(8,128)(2,1)} %copy.26), channel_id=1, source_target_pairs={{0,64},{1,65},{2,66},{3,67},{4,68},{5,69},{6,70},{7,71},{8,72},{9,... | collective-permute-start | bytes 2352008 | tf_op jit(solution)/shard_map/ppermute | solution.py:20
  19.3 45.6 %collective-permute-start.1 = (bf16[2,1,14,14,1000]{4,3,2,1,0:T(8,128)(2,1)}, bf16[2,1,14,14,1000]{4,3,2,1,0:T(8,128)(2,1)S(1)}, u32[]{:S(2)}, u32[]{:S(2)}) collective-permute-start(bf16[2,1,14,14,1000]{4,3,2,1,0:T(8,128)(2,1)} %copy.27), channel_id=1, source_target_pairs={{64,0},{65,1},{66,2},{67,3},{68,4},{69,5},{70,6},{71,7},{72,8},{73... | collective-permute-start | bytes 2352008 | tf_op jit(solution)/shard_map/ppermute | solution.py:23
  50.6 27.3 %copy-start.1 = (f32[3136,1000]{0,1:T(8,128)}, f32[3136,1000]{0,1:T(8,128)S(1)}, u32[]{:S(2)}) copy-start(f32[3136,1000]{0,1:T(8,128)S(1)} %get-tuple-element.22) | copy-start | bytes 37632004
  68.4 20.7 %collective-permute-start.2 = (bf16[2,10,1,14,1000]{4,3,2,1,0:T(8,128)(2,1)}, bf16[2,10,1,14,1000]{4,3,2,1,0:T(8,128)(2,1)S(1)}, u32[]{:S(2)}, u32[]{:S(2)}) collective-permute-start(bf16[2,10,1,14,1000]{4,3,2,1,0:T(8,128)(2,1)} %get-tuple-element.17), channel_id=1, source_target_pairs={{0,32},{1,33},{2,34},{3,35},{4,36},{5,37},{6,38},{7,39},{8,40},{9,... | collective-permute-start | bytes 1680008 | tf_op jit(solution)/shard_map/ppermute | solution.py:20
  74.5 20.3 %collective-permute-start.3 = (bf16[2,10,1,14,1000]{4,3,2,1,0:T(8,128)(2,1)}, bf16[2,10,1,14,1000]{4,3,2,1,0:T(8,128)(2,1)S(1)}, u32[]{:S(2)}, u32[]{:S(2)}) collective-permute-start(bf16[2,10,1,14,1000]{4,3,2,1,0:T(8,128)(2,1)} %get-tuple-element.18), channel_id=1, source_target_pairs={{32,0},{33,1},{34,2},{35,3},{36,4},{37,5},{38,6},{39,7},{40,8},{41... | collective-permute-start | bytes 1680008 | tf_op jit(solution)/shard_map/ppermute | solution.py:23
  78.0 45.1 %slice-start = ((s8[9175040]{0:T(1024)(128)(4,1)}), s8[4194304]{0:T(1024)(128)(4,1)S(1)}, s32[]{:S(2)}) async-start(s8[9175040]{0:T(1024)(128)(4,1)} %bitcast.6), calls=%async_computation.1 | async-start | bytes 8388608
  78.0 45.1 %slice-start.1 = ((s8[9175040]{0:T(1024)(128)(4,1)}), s8[4194304]{0:T(1024)(128)(4,1)S(1)}, s32[]{:S(2)}) async-start(s8[9175040]{0:T(1024)(128)(4,1)} %bitcast.6), calls=%async_computation.2 | async-start | bytes 8388608
  100.8 22.4 %slice-start.2 = ((s8[9175040]{0:T(1024)(128)(4,1)}), s8[786432]{0:T(1024)(128)(4,1)S(1)}, s32[]{:S(2)}) async-start(s8[9175040]{0:T(1024)(128)(4,1)} %bitcast.6), calls=%async_computation.3 | async-start | bytes 1572864
  101.0 16.8 %collective-permute-start.4 = (bf16[2,10,16,1,1000]{4,2,3,1,0:T(8,128)(2,1)S(1)}, bf16[2,10,16,1,1000]{4,2,3,1,0:T(8,128)(2,1)S(1)}, u32[]{:S(2)}, u32[]{:S(2)}) collective-permute-start(bf16[2,10,16,1,1000]{4,2,3,1,0:T(8,128)(2,1)S(1)} %copy.18), channel_id=1, source_target_pairs={{0,1},{1,2},{2,3},{3,4},{4,5},{5,6},{6,7},{7,8},{8,9},{9,10},{10,1... | collective-permute-start | bytes 1920008 | tf_op jit(solution)/shard_map/ppermute | solution.py:20
  104.5 17.4 %collective-permute-start.5 = (bf16[2,10,16,1,1000]{4,2,3,1,0:T(8,128)(2,1)S(1)}, bf16[2,10,16,1,1000]{4,2,3,1,0:T(8,128)(2,1)S(1)}, u32[]{:S(2)}, u32[]{:S(2)}) collective-permute-start(bf16[2,10,16,1,1000]{4,2,3,1,0:T(8,128)(2,1)S(1)} %copy.19), channel_id=1, source_target_pairs={{1,0},{2,1},{3,2},{4,3},{5,4},{6,5},{7,6},{8,7},{9,8},{10,9},{11,1... | collective-permute-start | bytes 1920008 | tf_op jit(solution)/shard_map/ppermute | solution.py:23
  197.9 8.3 %copy-start = (f32[3136,1000]{0,1:T(8,128)S(1)}, f32[3136,1000]{0,1:T(8,128)}, u32[]{:S(2)}) copy-start(f32[3136,1000]{0,1:T(8,128)} %copy.22) | copy-start | bytes 37632004
  215.5 2.7 copy-start.3
Sparse Core Ops, SparseCore 0:
  229.1 156.7 all-reduce.1
where the time goes:
time: 408 us; the launch traced here: 400 us
  local copies, waits for them, and re-layouts  102 us (25%)
  waiting for transfers between devices  85.9 us (21%)
  other arithmetic  76.5 us (19%)
  blocking collectives  68.8 us (17%)
  matrix products  34.1 us (8%)
  starting transfers between devices  16.6 us (4%)
  between operations  15.9 us (4%)
    psum x1, blocking collectives, local(): lax.psum((local_grad, piece_objective), ('ta', 'ha', 'wa'))  68.8 us
    psum x1, waiting for transfers between devices, local(): lax.psum((local_grad, piece_objective), ('ta', 'ha', 'wa'))  54.5 us
    unnamed x21, local copies, waits for them, and re-layouts  39.3 us
    div x2, local copies, waits for them, and re-layouts, local(): averaged_scores / sharpness_divisor  27.7 us
    add x2, other arithmetic, three_sum(): return first + middle + last  24.5 us
    ppermute x3, waiting for transfers between devices, with_halo(): lax.ppermute(lax.slice_in_dim(block, block.shape[dim] - width, None, axis...  22.9 us
    dot_general x1, matrix products, local(): lax.dot_general(score_slope, head_bf, (((1,), (1,)), ((), ())), preferred...  12.3 us
    dot_general x1, matrix products, local(): jnp.dot(feat_rows, head_bf, preferred_element_type=jnp.float32)  11.1 us
  transfers between devices with their start and end apart: 7, of which 5 were waited for; matrix products, arithmetic and copies ran while one was open for 20% of the time, Pallas kernels for 0%

commit v1 on v0

v1 whole, which is shorter than its diff:
```python
import functools

import jax
import jax.numpy as jnp
import numpy as np
from jax import lax
from jax.experimental import pallas as pl
from jax.experimental.pallas import tpu as pltpu
from jax.sharding import PartitionSpec as P

WW = 14
WV = 28
LR = 0.1
CLIP = 1000.0
LOG2E = 1.4426950408889634
LN2 = 0.6931471805599453
AXES = ("ta", "ha", "wa")
SWAP = [(0, 1), (1, 0)]


def clip_of(columns):
    return (columns + WV - WW // 2) // WV


def prep_kernel(rows, cols, steps, sel_ref, x_ref, out_ref, edge):
    step = pl.program_id(0)
    width = cols * 8
    for s in range(steps):

        @pl.when(step == s)
        def _(s=s):
            for i in range(rows):
                n = s * rows + i
                tile = jnp.dot(
                    sel_ref[...], x_ref[i * width : (i + 1) * width, :], preferred_element_type=jnp.float32
                )
                out_ref[n * 16 : (n + 1) * 16, :] = tile.astype(jnp.bfloat16)
                edge[n : n + 1, :] = tile[cols - 1 : cols]
                edge[32 + n : 33 + n, :] = tile[0:1]

    @pl.when(step == steps - 1)
    def _():
        total = steps * rows
        out_ref[total * 16 : total * 16 + 64, :] = edge[...].astype(jnp.bfloat16)


def student_kernel(chunk, f_ref, w_ref, zs_ref, s_ref):
    s_ref[...] = lax.dot_general(
        f_ref[...], w_ref[...], (((1,), (1,)), ((), ())), preferred_element_type=jnp.float32
    )

    def body(i, carry):
        at = pl.ds(pl.multiple_of(i * chunk, chunk), chunk)
        s = s_ref[at, :]
        z = (s - jnp.max(s, axis=1, keepdims=True)) * (0.5 * LOG2E)
        total = jnp.sum(jnp.exp2(z), axis=1, keepdims=True)
        zs_ref[at, :] = z - (jnp.log2(total) - 1.0)
        return carry

    lax.fori_loop(0, s_ref.shape[0] // chunk, body, 0)


def teacher_kernel(
    grid_h, rows, span, ha_ref, a_ref, x_ref, ext_ref, hm_ref, hx_ref, cw_ref, zs_ref, out_ref, kl_ref, sums
):
    half = pl.program_id(1)
    ha = ha_ref[0]
    per = rows // span
    a = a_ref[...]

    def pool(x, y):
        return jnp.dot(a, jnp.concatenate([x, y], axis=0), preferred_element_type=jnp.float32)

    def local(i):
        r = half * per - 1 + i
        x = x_ref[pl.ds(pl.multiple_of(r * 112, 16), 112), :]
        y = ext_ref[pl.ds(pl.multiple_of(r * 32, 16), 32), :]
        sums[i] = pool(x, y)

    for i in range(1, per + 1):
        local(i)
    for i, side, here in ((0, half == 0, ha == 1), (per + 1, half == span - 1, ha == 0)):

        @pl.when(jnp.logical_not(side))
        def _(i=i):
            local(i)

        @pl.when(jnp.logical_and(side, here))
        def _(i=i):
            sums[i] = pool(hm_ref[...], hx_ref[...])

        @pl.when(jnp.logical_and(side, jnp.logical_not(here)))
        def _(i=i):
            sums[i] = jnp.zeros(sums.shape[1:], jnp.float32)

    @pl.when(jnp.logical_and(pl.program_id(0) == 0, half == 0))
    def _():
        kl_ref[...] = jnp.zeros_like(kl_ref)

    def body(k, carry):
        at = pl.ds(pl.multiple_of(k * 112, 16), 112)
        row = ha * rows + half * per + k
        edge = jnp.logical_or(row == 0, row == grid_h - 1)
        scale = cw_ref[...] * jnp.where(edge, 1.0 / 2.0, 1.0 / 3.0)
        z = (sums[k] + sums[k + 1] + sums[k + 2]) * scale[:, 0:1]
        z = z - jnp.max(z, axis=1, keepdims=True)
        e = jnp.exp2(z)
        zs = zs_ref[at, :]
        total = jnp.sum(e, axis=1, keepdims=True)
        cross = jnp.sum(e * (z - zs), axis=1, keepdims=True)
        inv = 1.0 / total
        out_ref[at, :] = (jnp.exp2(zs) - e * (2.0 * inv)).astype(jnp.bfloat16)
        kl_ref[...] += jnp.broadcast_to(cross * inv - jnp.log2(total) + 1.0, kl_ref.shape)
        return carry

    lax.fori_loop(0, per, body, 0)


def local(features, teacher, head_weight):
    batch, frames, rows, columns, width = features.shape
    classes = teacher.shape[-1]
    n_wa = lax.axis_size("wa")
    grid_w = columns * n_wa
    grid_h = rows * lax.axis_size("ha")
    grid_t = frames * lax.axis_size("ta")
    ta, ha, wa = (lax.axis_index(name) for name in AXES)
    tokens = batch * rows * columns * frames
    group = columns * frames
    forward = [(i, i + 1) for i in range(n_wa - 1)]
    backward = [(i + 1, i) for i in range(n_wa - 1)]

    feat = features.transpose(0, 2, 3, 1, 4).reshape(tokens, width)
    teach5 = teacher.transpose(0, 2, 3, 1, 4)
    teach = teach5.reshape(tokens, classes)
    wt = head_weight.T
    wt_bf = wt.astype(jnp.bfloat16)

    edge_t = jnp.where(ta == 0, frames - 1, 0)
    pick = np.arange(16)[:, None] * frames
    sel = (jnp.arange(group)[None, :] == pick + edge_t).astype(jnp.bfloat16)

    k = np.arange(144)
    kw = np.where(k < 112, k // 8, np.where(k < 120, -1, np.where(k < 128, 14, k - 128)))
    kw = np.where(k == 142, -1, np.where(k == 143, 14, kw))
    kt = np.where(k < 112, k % 8, np.where(k < 128, (k - 112) % 8, 0))
    halo = k >= 128
    kt = jnp.where(halo, jnp.where(ta == 0, frames, -1), kt)[None, :]
    kw = kw[None, :]
    w = (np.arange(group) // frames)[:, None]
    t = (np.arange(group) % frames)[:, None]
    col, kcol = wa * columns + w, wa * columns + kw
    near = (abs(w - kw) <= 1) & (abs(t - kt) <= 1)
    ok = (kcol >= 0) & (kcol < grid_w) & (clip_of(kcol) == clip_of(col))
    pool = (near & ok).astype(jnp.bfloat16)
    left_ok = (col > 0) & (clip_of(col - 1) == clip_of(col))
    right_ok = (col < grid_w - 1) & (clip_of(col + 1) == clip_of(col))
    frame = ta * frames + t
    count = (3.0 - (frame == 0) - (frame == grid_t - 1)) * (1.0 + left_ok + right_ok)
    scale = jnp.broadcast_to((0.5 * LOG2E) / count.astype(jnp.float32), (group, 128))

    h_edge = jnp.where(ha == 0, rows - 1, 0)
    left = lax.ppermute(teach5[:, :, columns - 1], "wa", forward)
    right = lax.ppermute(teach5[:, :, 0], "wa", backward)
    h_main = lax.ppermute(lax.dynamic_index_in_dim(teach5, h_edge, 1, False), "ha", SWAP)
    steps = 4
    per = batch * rows // steps
    face = pl.pallas_call(
        functools.partial(prep_kernel, per, columns, steps),
        grid=(steps,),
        in_specs=[
            pl.BlockSpec((16, group), lambda i: (0, 0)),
            pl.BlockSpec((per * group, classes), lambda i: (i, 0)),
        ],
        out_specs=pl.BlockSpec((batch * rows * 16 + 64, classes), lambda i: (0, 0)),
        out_shape=jax.ShapeDtypeStruct((batch * rows * 16 + 64, classes), jnp.bfloat16),
        scratch_shapes=[pltpu.VMEM((64, classes), jnp.float32)],
        cost_estimate=pl.CostEstimate(flops=10**9, bytes_accessed=8 * 10**6, transcendentals=0),
    )(sel, teach)
    face = lax.ppermute(face, "ta", SWAP)
    n = batch * rows * 16
    corner_l = lax.ppermute(face[n : n + 32], "wa", forward)
    corner_r = lax.ppermute(face[n + 32 : n + 64], "wa", backward)
    ext = jnp.concatenate(
        [
            left,
            right,
            face[:n].reshape(batch, rows, 16, classes)[:, :, :columns],
            corner_l[: batch * rows].reshape(batch, rows, 1, classes),
            corner_r[: batch * rows].reshape(batch, rows, 1, classes),
        ],
        axis=2,
    )
    h_ext = lax.ppermute(lax.dynamic_index_in_dim(ext, h_edge, 1, False), "ha", SWAP)

    block = 448
    zs = pl.pallas_call(
        functools.partial(student_kernel, 112),
        grid=(tokens // block,),
        in_specs=[
            pl.BlockSpec((block, width), lambda i: (i, 0)),
            pl.BlockSpec((classes, width), lambda i: (0, 0)),
        ],
        out_specs=pl.BlockSpec((block, classes), lambda i: (i, 0)),
        out_shape=jax.ShapeDtypeStruct((tokens, classes), jnp.float32),
        scratch_shapes=[pltpu.VMEM((block, classes), jnp.float32)],
        cost_estimate=pl.CostEstimate(
            flops=2 * tokens * width * classes, bytes_accessed=22 * 10**6, transcendentals=tokens * classes
        ),
    )(feat, wt_bf)

    span = 2
    big = rows // span * group
    slope, kl = pl.pallas_call(
        functools.partial(teacher_kernel, grid_h, rows, span),
        grid=(batch, span),
        in_specs=[
            pl.BlockSpec(memory_space=pltpu.SMEM),
            pl.BlockSpec((group, 144), lambda b, s: (0, 0)),
            pl.BlockSpec((rows * group, classes), lambda b, s: (b, 0)),
            pl.BlockSpec((rows * 32, classes), lambda b, s: (b, 0)),
            pl.BlockSpec((group, classes), lambda b, s: (b, 0)),
            pl.BlockSpec((32, classes), lambda b, s: (b, 0)),
            pl.BlockSpec((group, 128), lambda b, s: (0, 0)),
            pl.BlockSpec((big, classes), lambda b, s: (b * span + s, 0)),
        ],
        out_specs=[
            pl.BlockSpec((big, classes), lambda b, s: (b * span + s, 0)),
            pl.BlockSpec((group, 128), lambda b, s: (0, 0)),
        ],
        out_shape=[
            jax.ShapeDtypeStruct((tokens, classes), jnp.bfloat16),
            jax.ShapeDtypeStruct((group, 128), jnp.float32),
        ],
        scratch_shapes=[pltpu.VMEM((rows // span + 2, group, classes), jnp.float32)],
        compiler_params=pltpu.CompilerParams(vmem_limit_bytes=48 * 2**20),
        cost_estimate=pl.CostEstimate(
            flops=4 * 10**9, bytes_accessed=27 * 10**6, transcendentals=2 * tokens * classes
        ),
    )(
        ha.astype(jnp.int32).reshape(1),
        pool,
        teach,
        ext.reshape(batch * rows * 32, classes),
        h_main.reshape(batch * group, classes),
        h_ext.reshape(batch * 32, classes),
        scale,
        zs,
    )

    n_dev = lax.axis_size(AXES)
    owned = width // n_dev
    head_part = lax.dot_general(feat, slope, (((0,), (0,)), ((), ())), preferred_element_type=jnp.float32)
    pieces = lax.all_to_all(
        head_part.astype(jnp.bfloat16).reshape(n_dev, owned, classes), AXES, 0, 0, tiled=True
    )
    feat_grad = jnp.dot(slope, wt_bf, preferred_element_type=jnp.float32).astype(jnp.bfloat16)
    feature_grad = feat_grad.reshape(batch, rows, columns, frames, width).transpose(0, 3, 1, 2, 4)

    mine = jnp.sum(pieces.astype(jnp.float32), axis=0)
    pair = jnp.stack([jnp.sum(mine * mine), jnp.sum(kl[:, 0])])
    pair = jnp.pad(pair, (0, 126)).reshape(1, 1, 128)
    pair = lax.all_to_all(jnp.broadcast_to(pair, (n_dev, 1, 128)), AXES, 0, 0, tiled=True)
    pair = jnp.sum(pair, axis=(0, 1))
    loss = pair[1] * (4.0 * LN2)
    clip = jnp.minimum(1.0, CLIP / (jnp.sqrt(pair[0]) + 1e-06))
    first = lax.axis_index(AXES) * owned
    weight_rows = lax.dynamic_slice_in_dim(head_weight, first, owned, 0)
    new_weight = weight_rows - LR * clip * mine
    return feature_grad, loss, new_weight


def solution(mesh):
    placed = P(None, "ta", "ha", "wa", None)
    return jax.shard_map(
        local,
        mesh=mesh,
        in_specs=(placed, placed, P()),
        out_specs=(placed, P(), P(AXES, None)),
        check_vma=False,
    )
```

time: 408 us -> 176 us (0.43); the launches traced: 400 us -> 175 us
  local copies, waits for them, and re-layouts: 102 us -> 19.9 us
  blocking collectives: 68.8 us -> 0 us
  other arithmetic: 76.5 us -> 11.8 us
  waiting for transfers between devices: 85.9 us -> 36.3 us
  Pallas kernels: 0 us -> 40.8 us
  starting transfers between devices: 16.6 us -> 39.5 us
  between operations: 15.9 us -> 3.28 us
  matrix products: 34.1 us -> 23.3 us
    psum x1 -> x0, blocking collectives: 68.8 us -> none  [local(): lax.psum((local_grad, piece_objective), ('ta', 'ha', 'wa'))]
    psum x1 -> x0, waiting for transfers between devices: 54.5 us -> none  [local(): lax.psum((local_grad, piece_objective), ('ta', 'ha', 'wa'))]
    pallas_call x0 -> x3, Pallas kernels: none -> 40.8 us  [the longest x1 18 us: local(): pl.pallas_call(functools.partial(student_kernel, 112), grid=(tokens // bl...]
    unnamed x21 -> x15, local copies, waits for them, and re-layouts: 39.3 us -> 4.44 us
    div x2 -> x0, local copies, waits for them, and re-layouts: 27.7 us -> none  [local(): averaged_scores / sharpness_divisor]
    all_to_all x0 -> x2, waiting for transfers between devices: none -> 26.3 us  [the longest x1 26.3 us: local(): lax.all_to_all(head_part.astype(jnp.bfloat16).reshape(n_dev, owned, class...]
    add x3 -> x0, other arithmetic: 24.5 us -> none  [the longest x2 24.5 us: three_sum(): return first + middle + last]
    all_to_all x0 -> x2, starting transfers between devices: none -> 23.4 us  [the longest x1 16.7 us: local(): lax.all_to_all(head_part.astype(jnp.bfloat16).reshape(n_dev, owned, class...]
  transfers between devices with their start and end apart: 7 -> 9, of which waited for: 5 -> 4; matrix products, arithmetic and copies ran while one was open for 20% -> 19% of each run, Pallas kernels for 0% -> 10%
where the time goes in v1:
time: 176 us; the launch traced here: 175 us
  Pallas kernels  40.8 us (23%)
  starting transfers between devices  39.5 us (22%)
  waiting for transfers between devices  36.3 us (21%)
  matrix products  23.3 us (13%)
  local copies, waits for them, and re-layouts  19.9 us (11%)
  other arithmetic  11.8 us (7%)
  between operations  3.28 us (2%)
    all_to_all x1, waiting for transfers between devices, local(): lax.all_to_all(head_part.astype(jnp.bfloat16).reshape(n_dev, owned, class...  26.3 us
    pallas_call x1, Pallas kernels, local(): pl.pallas_call(functools.partial(student_kernel, 112), grid=(tokens // bl...  18 us
    pallas_call x1, Pallas kernels, local(): pl.pallas_call(functools.partial(teacher_kernel, grid_h, rows, span), gri...  17.7 us
    all_to_all x1, starting transfers between devices, local(): lax.all_to_all(head_part.astype(jnp.bfloat16).reshape(n_dev, owned, class...  16.7 us
    dot_general x1, matrix products, local(): jnp.dot(slope, wt_bf, preferred_element_type=jnp.float32)  12.2 us
    dot_general x1, matrix products, local(): lax.dot_general(feat, slope, (((0,), (0,)), ((), ())), preferred_element_...  11.1 us
    all_to_all x1, starting transfers between devices, local(): lax.all_to_all(jnp.broadcast_to(pair, (n_dev, 1, 128)), AXES, 0, 0, tiled...  6.76 us
    pallas_call x1, Pallas kernels, local(): pl.pallas_call(functools.partial(prep_kernel, per, columns, steps), grid=...  5.11 us
  transfers between devices with their start and end apart: 9, of which 4 were waited for; matrix products, arithmetic and copies ran while one was open for 19% of the time, Pallas kernels for 10%

profile of v1, /device:TPU:1, one launch (start us, length us, event | category | flops | bytes accessed | tf_op | source)
XLA Modules:
  0.0 174.9 jit_solution(926926132167487523)
XLA Ops:
  0.6 0.7 add_bitcast_fusion
  1.3 0.7 fusion.4.sel_ref
  2.0 5.1 %shard_map.121 = bf16[512,1000]{1,0:T(8,128)(2,1)} custom-call(bf16[16,112]{1,0:T(8,128)(2,1)} %fusion.4.sel_ref, bf16[3136,1000]{1,0:T(8,128)(2,1)} %bitcast.53), custom_call_target="tpu_custom_call" | custom-call | flops 1000000000 | bytes 8000000 | tf_op jit(solution)/shard_map/pallas_call | solution.py:167
  7.1 1.5 copy.62
  8.6 1.5 collective-permute-start.2
  10.0 3.6 %copy.75 = bf16[2,8,14,14,1000]{4,1,2,0,3:T(8,128)(2,1)S(1)} copy(bf16[2,8,14,14,1000]{4,1,3,2,0:T(8,128)(2,1)} %param.11) | data formatting | bytes 12544000 | tf_op args[1]
  13.7 1.0 slice_bitcast_fusion
  14.7 4.1 %collective-permute-start = (bf16[2,14,8,1000]{3,2,1,0:T(8,128)(2,1)}, bf16[2,14,8,1000]{3,2,1,0:T(8,128)(2,1)}, u32[]{:S(2)}, u32[]{:S(2)}) collective-permute-start(bf16[2,14,8,1000]{3,2,1,0:T(8,128)(2,1)} %get-tuple-element.10), channel_id=1, source_target_pairs={{0,1},{1,2},{2,3},{3,4},{4,5},{5,6},{6,7},{7,8},{8,9},{9,10},{10,1... | collective-permute-start | bytes 1344008 | tf_op jit(solution)/shard_map/ppermute | solution.py:162
  18.7 1.3 collective-permute-start.1
  20.0 1.9 %dynamic-slice_bitcast_fusion = bf16[2,14,8,1000]{3,2,1,0:T(8,128)(2,1)} fusion(bf16[2,8,14,14,1000]{4,1,3,2,0:T(8,128)(2,1)} %param.11, s32[]{:T(128)S(6)} %select_n.44), kind=kLoop, calls=%fused_computation.8 | loop fusion | bytes 896004 | tf_op jit(solution)/shard_map/jit(dynamic_index_in_dim)/squeeze | solution.py:164
  21.9 3.6 %collective-permute-start.5 = (bf16[2,14,8,1000]{3,2,1,0:T(8,128)(2,1)}, bf16[2,14,8,1000]{3,2,1,0:T(8,128)(2,1)S(1)}, u32[]{:S(2)}, u32[]{:S(2)}) collective-permute-start(bf16[2,14,8,1000]{3,2,1,0:T(8,128)(2,1)} %dynamic-slice_bitcast_fusion), channel_id=1, source_target_pairs={{0,32},{32,0},{1,33},{33,1},{2,34},{34,2},{3,35},{35,3},{4,36},{36... | collective-permute-start | bytes 1344008 | tf_op jit(solution)/shard_map/ppermute | solution.py:164
  25.5 3.8 %convert_bitcast_fusion.1.w_ref = bf16[1000,1024]{1,0:T(8,128)(2,1)} fusion(f32[1024,1000]{0,1:T(8,128)} %param.12), kind=kLoop, calls=%fused_computation.5 | loop fusion | flops 1024000 | bytes 6144000 | tf_op jit(solution)/shard_map/convert_element_type | solution.py:136
  29.3 0.6 broadcast_select_fusion
  29.9 0.6 and_select_fusion
  30.4 18.0 %shard_map.122.zs_ref = f32[3136,1000]{1,0:T(8,128)} custom-call(bf16[3136,1024]{1,0:T(8,128)(2,1)} %bitcast.64, bf16[1000,1024]{1,0:T(8,128)(2,1)} %convert_bitcast_fusion.1.w_ref), custom_call_target="tpu_custom_call" | custom-call | flops 6422528000 | bytes 22000000 | tf_op jit(solution)/shard_map/pallas_call | solution.py:196
  48.4 0.6 fusion.9
  49.0 0.2 fusion.12
  49.2 4.0 %collective-permute-start.3 = (bf16[32,1000]{0,1:T(8,128)(2,1)S(1)}, bf16[32,1000]{0,1:T(8,128)(2,1)S(1)}, u32[]{:S(2)}, u32[]{:S(2)}) collective-permute-start(bf16[32,1000]{0,1:T(8,128)(2,1)S(1)} %get-tuple-element.12), channel_id=1, source_target_pairs={{0,1},{1,2},{2,3},{3,4},{4,5},{5,6},{6,7},{7,8},{8,9},{9,10},{10,1... | collective-permute-start | bytes 192008 | tf_op jit(solution)/shard_map/ppermute | solution.py:181
  53.2 1.3 collective-permute-start.4
  54.5 0.5 and_reduce_fusion
  55.1 0.7 copy.72
  55.7 2.1 %collective-permute-done.3 = bf16[32,1000]{0,1:T(8,128)(2,1)S(1)} collective-permute-done((bf16[32,1000]{0,1:T(8,128)(2,1)S(1)}, bf16[32,1000]{0,1:T(8,128)(2,1)S(1)}, u32[]{:S(2)}, u32[]{:S(2)}) %collective-permute-start.3) | collective-permute-done | bytes 64032 | tf_op jit(solution)/shard_map/ppermute | solution.py:181
  57.9 0.2 copy.64
  58.0 0.1 reshape.66
  58.1 3.6 %collective-permute-done.4 = bf16[32,1000]{0,1:T(8,128)(2,1)S(1)} collective-permute-done((bf16[32,1000]{0,1:T(8,128)(2,1)S(1)}, bf16[32,1000]{0,1:T(8,128)(2,1)S(1)}, u32[]{:S(2)}, u32[]{:S(2)}) %collective-permute-start.4) | collective-permute-done | bytes 64032 | tf_op jit(solution)/shard_map/ppermute | solution.py:182
  61.7 0.2 copy.65
  61.9 0.1 reshape.67
  62.0 4.7 %concatenate.3 = bf16[2,14,32,1000]{3,2,1,0:T(8,128)(2,1)S(1)} concatenate(bf16[2,14,8,1000]{3,2,1,0:T(8,128)(2,1)} %collective-permute-done, bf16[2,14,8,1000]{3,2,1,0:T(8,128)(2,1)} %collective-permute-done.1, bf16[2,14,14,1000]{3,2,1,0:T(8,128)(2,1)S(1)} %bitcast.57, bf16[2,14,1,1000]{3,2,1,0:T(2,128)(2,1)S(1)} %reshape.66, bf16[2,14,1,1000]{3,2,1,0:T(2,128)(2,1)S(1)} %reshape.67), dimensions={2} | concatenate | bytes 3584000 | tf_op jit(solution)/shard_map/concatenate | solution.py:183
  66.7 0.4 collective-permute-start.6
  67.1 0.8 fusion.3.a_ref
  67.9 4.2 %collective-permute-done.6 = bf16[2,32,1000]{2,1,0:T(8,128)(2,1)S(1)} collective-permute-done((bf16[2,32,1000]{2,1,0:T(8,128)(2,1)S(1)}, bf16[2,32,1000]{2,1,0:T(8,128)(2,1)S(1)}, u32[]{:S(2)}, u32[]{:S(2)}) %collective-permute-start.6) | collective-permute-done | bytes 128032 | tf_op jit(solution)/shard_map/ppermute | solution.py:193
  72.1 0.7 broadcast_in_dim.20.cw_ref
  72.9 17.7 %shard_map.123 = (bf16[3136,1000]{1,0:T(8,128)(2,1)}, f32[112,128]{1,0:T(8,128)S(1)}) custom-call(s32[1]{0:T(128)} %bitcast.ha_ref, bf16[112,144]{1,0:T(8,128)(2,1)S(1)} %fusion.3.a_ref, bf16[3136,1000]{1,0:T(8,128)(2,1)} %bitcast.54, bf16[896,1000]{1,0:T(8,128)(2,1)S(1)} %bitcast.50, bf16[224,1000]{1,0:T(8,128)(2,1)S(1)} %bitcast.51, ...), custom_call_target="tpu_custom_call" | custom-call | flops 4000000000 | bytes 27000000 | tf_op jit(solution)/shard_map/pallas_call | solution.py:213
  90.6 11.1 %convert_bitcast_fusion = bf16[1024,1000]{0,1:T(8,128)(2,1)S(1)} fusion(bf16[3136,1000]{1,0:T(8,128)(2,1)} %get-tuple-element.5, bf16[3136,1024]{1,0:T(8,128)(2,1)} %bitcast.65), kind=kOutput, calls=%fused_computation.3 | convolution fusion | flops 6423552000 | bytes 14742528 | tf_op jit(solution)/shard_map/dot_general | solution.py:252
  101.7 2.6 %copy.68 = bf16[1024,1000]{1,0:T(8,128)(2,1)} copy(bf16[1024,1000]{0,1:T(8,128)(2,1)S(1)} %convert_bitcast_fusion) | data formatting | bytes 4096000 | tf_op jit(solution)/shard_map/convert_element_type | solution.py:254
  104.3 16.7 %all-to-all-start = ((bf16[128,8,1000]{2,1,0:T(8,128)(2,1)}), bf16[128,8,1000]{2,1,0:T(8,128)(2,1)S(1)}, u32[]{:S(2)}, u32[]{:S(2)}) async-start(bf16[128,8,1000]{2,1,0:T(8,128)(2,1)} %bitcast.56), calls=%async_computation | async-start | bytes 4194304 | tf_op jit(solution)/shard_map/all_to_all | solution.py:253
  121.0 1.2 constant_dynamic-slice_fusion
  122.2 0.2 copy.73
  122.4 0.6 slice_reduce_fusion
  123.0 26.3 %all-to-all-done = bf16[128,8,1000]{2,1,0:T(8,128)(2,1)S(1)} async-done(((bf16[128,8,1000]{2,1,0:T(8,128)(2,1)}), bf16[128,8,1000]{2,1,0:T(8,128)(2,1)S(1)}, u32[]{:S(2)}, u32[]{:S(2)}) %all-to-all-start) | async-done | bytes 2048032 | tf_op jit(solution)/shard_map/all_to_all | solution.py:253
  149.3 0.4 convert_reduce_fusion
  149.7 0.6 multiply_reduce_fusion
  150.3 1.4 fusion.10
  151.6 0.7 broadcast_in_dim.21
  152.3 6.8 %all-to-all-start.1 = ((f32[128,1,128]{2,1,0:T(1,128)}), f32[128,1,128]{2,1,0:T(1,128)S(1)}, u32[]{:S(2)}, u32[]{:S(2)}) async-start(f32[128,1,128]{2,1,0:T(1,128)} %broadcast_in_dim.21), calls=%async_computation.1 | async-start | bytes 131072 | tf_op jit(solution)/shard_map/all_to_all | solution.py:262
  159.1 12.2 %convolution_convert_fusion = bf16[3136,1024]{1,0:T(8,128)(2,1)} fusion(bf16[3136,1000]{1,0:T(8,128)(2,1)} %get-tuple-element.5, f32[1024,1000]{0,1:T(8,128)} %param.12), kind=kOutput, calls=%fused_computation | convolution fusion | flops 6426763264 | bytes 16790528 | tf_op jit(solution)/shard_map/dot_general | solution.py:256
  171.3 0.6 fusion.13
  172.6 0.6 multiply_subtract_fusion
  (19 shorter events, 0.1 us)
Async XLA Ops:
  8.6 40.4 %collective-permute-start.2 = (bf16[512,1000]{0,1:T(8,128)(2,1)S(1)}, bf16[512,1000]{0,1:T(8,128)(2,1)S(1)}, u32[]{:S(2)}, u32[]{:S(2)}) collective-permute-start(bf16[512,1000]{0,1:T(8,128)(2,1)S(1)} %copy.62), channel_id=1, source_target_pairs={{0,64},{64,0},{1,65},{65,1},{2,66},{66,2},{3,67},{67,3},{4,68},{68... | collective-permute-start | bytes 3072008 | tf_op jit(solution)/shard_map/ppermute | solution.py:179
  13.6 15.6 %copy-start.2 = (s32[144]{0:T(256)S(1)}, s32[144]{0:T(256)}, u32[]{:S(2)}) copy-start(s32[144]{0:T(256)} %constant.131.clone) | copy-start | bytes 1732
  13.6 15.6 %copy-start.5 = (pred[144]{0:T(512)(128)(4,1)S(1)}, pred[144]{0:T(512)(128)(4,1)}, u32[]{:S(2)}) copy-start(pred[144]{0:T(512)(128)(4,1)} %constant.130.clone) | copy-start | bytes 436
  13.6 16.2 %copy-start.1 = (s32[1,144]{1,0:T(1,128)S(1)}, s32[1,144]{1,0:T(1,128)}, u32[]{:S(2)}) copy-start(s32[1,144]{1,0:T(1,128)} %constant.133.clone) | copy-start | bytes 1732
  14.7 47.3 %collective-permute-start = (bf16[2,14,8,1000]{3,2,1,0:T(8,128)(2,1)}, bf16[2,14,8,1000]{3,2,1,0:T(8,128)(2,1)}, u32[]{:S(2)}, u32[]{:S(2)}) collective-permute-start(bf16[2,14,8,1000]{3,2,1,0:T(8,128)(2,1)} %get-tuple-element.10), channel_id=1, source_target_pairs={{0,1},{1,2},{2,3},{3,4},{4,5},{5,6},{6,7},{7,8},{8,9},{9,10},{10,1... | collective-permute-start | bytes 1344008 | tf_op jit(solution)/shard_map/ppermute | solution.py:162
  18.7 43.3 %collective-permute-start.1 = (bf16[2,14,8,1000]{3,2,1,0:T(8,128)(2,1)}, bf16[2,14,8,1000]{3,2,1,0:T(8,128)(2,1)}, u32[]{:S(2)}, u32[]{:S(2)}) collective-permute-start(bf16[2,14,8,1000]{3,2,1,0:T(8,128)(2,1)} %get-tuple-element.9), channel_id=1, source_target_pairs={{1,0},{2,1},{3,2},{4,3},{5,4},{6,5},{7,6},{8,7},{9,8},{10,9},{11,1... | collective-permute-start | bytes 1344008 | tf_op jit(solution)/shard_map/ppermute | solution.py:163
  21.9 46.0 %collective-permute-start.5 = (bf16[2,14,8,1000]{3,2,1,0:T(8,128)(2,1)}, bf16[2,14,8,1000]{3,2,1,0:T(8,128)(2,1)S(1)}, u32[]{:S(2)}, u32[]{:S(2)}) collective-permute-start(bf16[2,14,8,1000]{3,2,1,0:T(8,128)(2,1)} %dynamic-slice_bitcast_fusion), channel_id=1, source_target_pairs={{0,32},{32,0},{1,33},{33,1},{2,34},{34,2},{3,35},{35,3},{4,36},{36... | collective-permute-start | bytes 1344008 | tf_op jit(solution)/shard_map/ppermute | solution.py:164
  30.4 18.0 %copy-start.3 = (s32[112,1]{0,1:T(1,128)S(1)}, s32[112,1]{0,1:T(1,128)}, u32[]{:S(2)}) copy-start(s32[112,1]{0,1:T(1,128)} %constant.132.clone) | copy-start | bytes 1348
  30.4 18.0 %copy-start.4 = (s32[112,1]{0,1:T(1,128)S(1)}, s32[112,1]{0,1:T(1,128)}, u32[]{:S(2)}) copy-start(s32[112,1]{0,1:T(1,128)} %constant.134.clone) | copy-start | bytes 1348
  48.4 18.7 %copy-start = (pred[112,144]{1,0:T(8,128)(4,1)S(1)}, pred[112,144]{1,0:T(8,128)(4,1)}, u32[]{:S(2)}) copy-start(pred[112,144]{1,0:T(8,128)(4,1)} %constant.142) | copy-start | bytes 48388
  49.2 8.7 %collective-permute-start.3 = (bf16[32,1000]{0,1:T(8,128)(2,1)S(1)}, bf16[32,1000]{0,1:T(8,128)(2,1)S(1)}, u32[]{:S(2)}, u32[]{:S(2)}) collective-permute-start(bf16[32,1000]{0,1:T(8,128)(2,1)S(1)} %get-tuple-element.12), channel_id=1, source_target_pairs={{0,1},{1,2},{2,3},{3,4},{4,5},{5,6},{6,7},{7,8},{8,9},{9,10},{10,1... | collective-permute-start | bytes 192008 | tf_op jit(solution)/shard_map/ppermute | solution.py:181
  53.2 8.5 %collective-permute-start.4 = (bf16[32,1000]{0,1:T(8,128)(2,1)S(1)}, bf16[32,1000]{0,1:T(8,128)(2,1)S(1)}, u32[]{:S(2)}, u32[]{:S(2)}) collective-permute-start(bf16[32,1000]{0,1:T(8,128)(2,1)S(1)} %get-tuple-element.11), channel_id=1, source_target_pairs={{1,0},{2,1},{3,2},{4,3},{5,4},{6,5},{7,6},{8,7},{9,8},{10,9},{11,1... | collective-permute-start | bytes 192008 | tf_op jit(solution)/shard_map/ppermute | solution.py:182
  66.7 5.4 %collective-permute-start.6 = (bf16[2,32,1000]{2,1,0:T(8,128)(2,1)S(1)}, bf16[2,32,1000]{2,1,0:T(8,128)(2,1)S(1)}, u32[]{:S(2)}, u32[]{:S(2)}) collective-permute-start(bf16[2,32,1000]{2,1,0:T(8,128)(2,1)S(1)} %dynamic-slice_bitcast_fusion.1), channel_id=1, source_target_pairs={{0,32},{32,0},{1,33},{33,1},{2,34},{34,2},{3,35},{35,3},{4,36},{36... | collective-permute-start | bytes 384008 | tf_op jit(solution)/shard_map/ppermute | solution.py:193
  104.3 45.0 %all-to-all-start = ((bf16[128,8,1000]{2,1,0:T(8,128)(2,1)}), bf16[128,8,1000]{2,1,0:T(8,128)(2,1)S(1)}, u32[]{:S(2)}, u32[]{:S(2)}) async-start(bf16[128,8,1000]{2,1,0:T(8,128)(2,1)} %bitcast.56), calls=%async_computation | async-start | bytes 4194304 | tf_op jit(solution)/shard_map/all_to_all | solution.py:253
  152.3 19.0 %all-to-all-start.1 = ((f32[128,1,128]{2,1,0:T(1,128)}), f32[128,1,128]{2,1,0:T(1,128)S(1)}, u32[]{:S(2)}, u32[]{:S(2)}) async-start(f32[128,1,128]{2,1,0:T(1,128)} %broadcast_in_dim.21), calls=%async_computation.1 | async-start | bytes 131072 | tf_op jit(solution)/shard_map/all_to_all | solution.py:262
